TPU v7x, 32 devices: a whole 2x2x4 slice. The times are simulated.
32 devices in a mesh: slides: 2 (over y), seq: 4 (over z), sub: 4 (over x, core).
Axes of the slice: x: 2, y: 2, z: 4, core: 2. Of those that a mesh axis runs over, the one named last changes fastest.
Arguments:
- q_heads: bfloat16 [8192, 768], P(('slides', 'seq'), 'sub'), parts along dimension 0, may hold values from -8 to 8
- k_heads: bfloat16 [8192, 768], P(('slides', 'seq'), 'sub'), parts along dimension 0, may hold values from -8 to 8
- v_heads: bfloat16 [8192, 768], P(('slides', 'seq'), 'sub'), parts along dimension 0, may hold values from -6 to 6
- w_out: bfloat16 [768, 768], replicated, may hold values from -0.21875 to 0.21875
- offsets: int32 [2, 16], replicated, may hold values from 0 to 15, as said below
- valid: int32 [2], P('slides'), parts along dimension 0, may hold values from 3073 to 4096
Outputs:
- mixed: bfloat16 [8192, 768], P(('slides', 'seq'), 'sub'), parts along dimension 0
There are 2 independent parts, one for each index of `slides`. A program takes and returns all parts, laid end to end along the dimension named above; an argument that names none is the same for every part. Nothing has to cross between parts.
Inputs may be any that keep to these rules, and one draw needn't show every extreme that they name: `offsets`: row 0 lies below 4, row 1 below 16. Tiles at positions valid[0] and beyond are padding.
All inputs are finite; a program needn't handle non-finite values.
Results may differ from a plain program's by a relative error of at most 0.012.
Values may be sent and summed in bfloat16 or wider, within the bound.
A program may use at most 64 MiB of HBM per device.

v0:
```python
import jax
import jax.numpy as jnp
from jax import lax
from jax.sharding import PartitionSpec as P

HS = 48
GROUP = 4
R1 = 4
R2 = 16
NEG_FILL = -1e30


def swapped(value, axis, stride):
    mask = 2**stride
    pairs = [(source, source ^ mask) for source in range(lax.axis_size(axis))]
    return lax.ppermute(value, axis, pairs)


def pick_rows(source, stride, chosen):
    grouped = source.reshape(source.shape[0] // stride, stride, source.shape[1], source.shape[2])
    onehot = jnp.arange(stride, dtype=jnp.int32)[:, None] == chosen[None, :]
    return jnp.sum(
        jnp.where(onehot[None, :, :, None], grouped, jnp.zeros((), source.dtype)), axis=1
    )


def spread_back(maxima, totals, numer, stride, chosen):
    onehot = (jnp.arange(stride, dtype=jnp.int32)[:, None] == chosen[None, :])[None]
    count = maxima.shape[0] * stride
    full_max = jnp.where(onehot, maxima[:, None, :], NEG_FILL).reshape(count, maxima.shape[1])
    full_tot = jnp.where(onehot, totals[:, None, :], 0.0).reshape(count, maxima.shape[1])
    full_num = jnp.where(onehot[..., None], numer[:, None, :, :], 0.0).reshape(
        count, numer.shape[1], numer.shape[2]
    )
    return (full_max, full_tot, full_num)


def block_stats(q_sel, k_sel, v_sel, live):
    n_query = q_sel.shape[0]
    width = min(512, n_query)
    live_rows = live.T[:, None, :]

    def attend(q_blk):
        scores = jnp.einsum(
            "qhd,khd->hqk", q_blk, k_sel, preferred_element_type=jnp.float32
        ) * HS ** (-0.5)
        scores = jnp.where(live_rows, scores, NEG_FILL)
        peak = jnp.max(scores, axis=2)
        probs = jnp.exp(scores - peak[:, :, None])
        mass = jnp.sum(probs, axis=2)
        weighted = jnp.einsum(
            "hqk,khd->qhd", probs.astype(jnp.bfloat16), v_sel, preferred_element_type=jnp.float32
        )
        return (peak.T, mass.T, weighted)

    peak, mass, weighted = lax.map(
        attend, q_sel.reshape(n_query // width, width, q_sel.shape[1], q_sel.shape[2])
    )
    return (
        peak.reshape(n_query, q_sel.shape[1]),
        mass.reshape(n_query, q_sel.shape[1]),
        weighted.reshape(n_query, q_sel.shape[1], q_sel.shape[2]),
    )


def local(q_heads, k_heads, v_heads, w_out, offsets, valid):
    tok_rows = q_heads.shape[0]
    head_cols = q_heads.shape[1]
    local_heads = head_cols // HS
    seq_index = lax.axis_index("seq")
    sub_index = lax.axis_index("sub")
    block_start = seq_index * tok_rows
    mine = lax.dynamic_slice_in_dim(offsets, sub_index * local_heads, local_heads, 1)
    limit = valid[0]
    queries = q_heads.reshape(tok_rows, local_heads, HS)
    keys_local = k_heads.reshape(tok_rows, local_heads, HS)
    values_local = v_heads.reshape(tok_rows, local_heads, HS)
    own_rows = jnp.arange(tok_rows, dtype=jnp.int32)
    live_near = jnp.broadcast_to((block_start + own_rows < limit)[:, None], (tok_rows, local_heads))
    near = block_stats(queries, keys_local, values_local, live_near)
    middle_offs = mine[0]
    middle_rows = tok_rows // R1
    q_middle = pick_rows(queries, R1, middle_offs)
    kv_middle = jnp.concatenate(
        [
            pick_rows(keys_local, R1, middle_offs).reshape(middle_rows, head_cols),
            pick_rows(values_local, R1, middle_offs).reshape(middle_rows, head_cols),
        ],
        axis=1,
    )
    block_ids = seq_index.reshape(1)
    for bit_index in range(GROUP.bit_length() - 1):
        partner = swapped(kv_middle, "seq", bit_index)
        kv_middle = jnp.concatenate([kv_middle, partner], axis=0)
        block_ids = jnp.concatenate([block_ids, block_ids ^ 1 << bit_index])
    middle_pos = (
        block_ids[:, None] * tok_rows + jnp.arange(middle_rows, dtype=jnp.int32)[None, :] * R1
    )
    live_middle = middle_pos.reshape(-1, 1) + middle_offs[None, :] < limit
    middle_count = kv_middle.shape[0]
    middle = block_stats(
        q_middle,
        kv_middle[:, :head_cols].reshape(middle_count, local_heads, HS),
        kv_middle[:, head_cols:].reshape(middle_count, local_heads, HS),
        live_middle,
    )
    middle = spread_back(middle[0], middle[1], middle[2], R1, middle_offs)
    wide_offs = mine[1]
    wide_rows = tok_rows // R2
    q_wide = pick_rows(queries, R2, wide_offs)
    kv_wide = jnp.concatenate(
        [
            pick_rows(keys_local, R2, wide_offs).reshape(wide_rows, head_cols),
            pick_rows(values_local, R2, wide_offs).reshape(wide_rows, head_cols),
        ],
        axis=1,
    )
    piece = lax.all_gather(kv_wide, "seq", axis=0, tiled=True)
    run_peak = jnp.full((wide_rows, local_heads), NEG_FILL, jnp.float32)
    piece_len = piece.shape[0]
    global_row = jnp.arange(piece_len, dtype=jnp.int32)
    position = global_row // wide_rows * tok_rows + global_row % wide_rows * R2
    live_piece = position[:, None] + wide_offs[None, :] < limit
    piece_peak, piece_mass, piece_num = block_stats(
        q_wide,
        piece[:, :head_cols].reshape(piece_len, local_heads, HS),
        piece[:, head_cols:].reshape(piece_len, local_heads, HS),
        live_piece,
    )
    new_peak = jnp.maximum(run_peak, piece_peak)
    new_scale = jnp.exp(piece_peak - new_peak)
    wide = (new_peak, new_scale * piece_mass, new_scale[..., None] * piece_num)
    wide = spread_back(wide[0], wide[1], wide[2], R2, wide_offs)
    top = jnp.maximum(jnp.maximum(near[0], middle[0]), wide[0])
    denom = jnp.zeros_like(top)
    numer = jnp.zeros_like(near[2])
    for peak, mass, partial_num in (near, middle, wide):
        weight = jnp.exp(peak - top)
        denom = denom + weight * mass
        numer = numer + weight[..., None] * partial_num
    attn = (numer / denom[..., None]).reshape(tok_rows, head_cols).astype(jnp.bfloat16)
    w_cols = lax.dynamic_slice_in_dim(w_out, sub_index * head_cols, head_cols, 1)
    projected = jnp.dot(
        lax.all_gather(attn, "sub", axis=1, tiled=True), w_cols, preferred_element_type=jnp.float32
    )
    keep = block_start + own_rows < limit
    return jnp.where(keep[:, None], projected, 0.0).astype(jnp.bfloat16)


def solution(mesh):
    placed = (
        P(("slides", "seq"), "sub"),
        P(("slides", "seq"), "sub"),
        P(("slides", "seq"), "sub"),
        P(),
        P(),
        P("slides"),
    )
    return jax.shard_map(
        local, mesh=mesh, in_specs=placed, out_specs=P(("slides", "seq"), "sub"), check_vma=False
    )
```

profile of v0, /device:TPU:0, one launch (start us, length us, event | category | flops | bytes accessed | tf_op | source)
XLA Modules:
  0.0 160.5 jit_solution(14482707209866753938)
XLA Ops:
  11.0 1.5 reshape_reshape.22
  12.5 1.5 reshape_reshape.23
  14.1 1.5 reshape_reshape.24
  15.6 6.2 %select_reduce_fusion.5 = (bf16[256,4,48]{2,1,0:T(4,128)(2,1)}, bf16[256,4,48]{2,1,0:T(4,128)(2,1)}, bf16[256,4,48]{2,1,0:T(4,128)(2,1)}) fusion(bf16[256,4,4,48]{3,2,1,0:T(4,128)(2,1)} %reshape_reshape.22, pred[4,4]{1,0:T(4,128)(4,1)S(1)} %iota_compare_fusion.1, bf16[256,4,4,48]{3,2,1,0:T(4,128)(2,1)} %reshape_reshape.23, ...), kind=kLoop, calls=%fused_computation.36 | loop fusion | flops 1032192 | bytes 1474576 | tf_op jit(solution)/shard_map/reduce_sum | solution.py:22
  21.8 1.8 %copy.50 = bf16[256,4,48]{0,2,1:T(8,128)(2,1)} copy(bf16[256,4,48]{2,1,0:T(4,128)(2,1)} %get-tuple-element.148) | data formatting | bytes 196608 | tf_op jit(solution)/shard_map/reduce_sum | solution.py:22
  23.6 1.7 %copy.48 = bf16[256,4,48]{0,2,1:T(8,128)(2,1)} copy(bf16[256,4,48]{2,1,0:T(4,128)(2,1)} %get-tuple-element.147) | data formatting | bytes 196608 | tf_op jit(solution)/shard_map/reduce_sum | solution.py:22
  25.4 1.6 %pad_maximum_fusion.2 = bf16[256,384]{0,1:T(8,128)(2,1)} fusion(bf16[256,192]{0,1:T(8,128)(2,1)} %bitcast.123, bf16[256,192]{0,1:T(8,128)(2,1)} %bitcast.126), kind=kLoop, calls=%fused_computation.52 | loop fusion | flops 393216 | bytes 393216 | tf_op jit(solution)/shard_map/concatenate | solution.py:84
  27.0 3.1 %collective-permute-start = (bf16[256,384]{0,1:T(8,128)(2,1)}, bf16[256,384]{0,1:T(8,128)(2,1)}, u32[]{:S(2)}, u32[]{:S(2)}) collective-permute-start(bf16[256,384]{0,1:T(8,128)(2,1)} %pad_maximum_fusion.2), channel_id=1, source_target_pairs={{0,4},{4,0},{8,12},{12,8},{1,5},{5,1},{9,13},{13,9},{2,6},{6,2},{1... | collective-permute-start | bytes 589832 | tf_op jit(solution)/shard_map/ppermute | solution.py:16
  31.1 1.5 reshape_reshape.25
  32.6 1.5 reshape_reshape.26
  34.1 1.5 reshape_reshape.27
  36.5 28.2 %while.3 = (s32[]{:T(128)}, f32[2,512,4]{1,2,0:T(4,128)}, f32[2,512,4]{1,2,0:T(4,128)}, f32[2,512,4,48]{1,0,3,2:T(2,128)}, bf16[2,512,4,48]{1,3,2,0:T(8,128)(2,1...) while((s32[]{:T(128)}, f32[2,512,4]{1,2,0:T(4,128)}, ...), condition=%wide.region_3.4_spmd.clone, body=%wide.region_0.3_spmd.clone.sunk | while | flops 425717760 | bytes 30018820 | solution.py:56
  38.2 2.1 %fusion.69 = f32[4,512]{1,0:T(4,128)S(1)} fusion(f32[4,512,1024]{2,1,0:T(8,128)S(1)} %get-tuple-element.239, f32[4,512]{1,0:T(4,128)S(1)} %get-tuple-element.240, pred[1024]{0:T(1024)(128)(4,1)S(1)} %get-tuple-element.270), kind=kLoop, calls=%fused_computation.5.clone.1 | loop fusion | flops 8386560 | bytes 8406016 | tf_op jit(solution)/shard_map/while/body/eval_jaxpr/reduce_sum | solution.py:50
  40.3 1.8 %fusion.70 = f32[1,512,4,48]{1,3,2,0:T(8,128)S(1)} fusion(bf16[1024,4,48]{0,2,1:T(8,128)(2,1)S(1)} %copy-done.10, f32[4,512,1024]{2,1,0:T(8,128)S(1)} %get-tuple-element.239, f32[4,512]{1,0:T(4,128)S(1)} %get-tuple-element.240, pred[1024]{0:T(1024)(128)(4,1)S(1)} %get-tuple-element.270), kind=kOutput, calls=%fused_computation.8.clone.1 | convolution fusion | flops 209715200 | bytes 9184256 | tf_op jit(solution)/shard_map/while/body/eval_jaxpr/hqk,khd->qhd/dot_general | solution.py:51
  42.6 8.1 %dynamic_update_slice.35 = f32[2,512,4,48]{1,0,3,2:T(2,128)} dynamic-update-slice(f32[2,512,4,48]{1,0,3,2:T(2,128)} %get-tuple-element.256, f32[1,512,4,48]{1,0,3,2:T(1,128)S(1)} %copy.83, s32[]{:T(128)S(6)} %copy.91, s32[]{:T(128)} %constant.119.clone.1..sunk, s32[]{:T(128)} %constant.119.clone.1..sunk, s32[]{:T(128)} %constant.119.clone.1..sunk) | dynamic-update-slice | bytes 786436 | tf_op jit(solution)/shard_map/while/body/jit(dynamic_update_index_in_dim)/dynamic_update_slice | solution.py:56
  52.2 2.1 %fusion.69 = f32[4,512]{1,0:T(4,128)S(1)} fusion(f32[4,512,1024]{2,1,0:T(8,128)S(1)} %get-tuple-element.239, f32[4,512]{1,0:T(4,128)S(1)} %get-tuple-element.240, pred[1024]{0:T(1024)(128)(4,1)S(1)} %get-tuple-element.270), kind=kLoop, calls=%fused_computation.5.clone.1 | loop fusion | flops 8386560 | bytes 8406016 | tf_op jit(solution)/shard_map/while/body/eval_jaxpr/reduce_sum | solution.py:50
  54.4 1.8 %fusion.70 = f32[1,512,4,48]{1,3,2,0:T(8,128)S(1)} fusion(bf16[1024,4,48]{0,2,1:T(8,128)(2,1)S(1)} %copy-done.10, f32[4,512,1024]{2,1,0:T(8,128)S(1)} %get-tuple-element.239, f32[4,512]{1,0:T(4,128)S(1)} %get-tuple-element.240, pred[1024]{0:T(1024)(128)(4,1)S(1)} %get-tuple-element.270), kind=kOutput, calls=%fused_computation.8.clone.1 | convolution fusion | flops 209715200 | bytes 9184256 | tf_op jit(solution)/shard_map/while/body/eval_jaxpr/hqk,khd->qhd/dot_general | solution.py:51
  56.6 8.1 %dynamic_update_slice.35 = f32[2,512,4,48]{1,0,3,2:T(2,128)} dynamic-update-slice(f32[2,512,4,48]{1,0,3,2:T(2,128)} %get-tuple-element.256, f32[1,512,4,48]{1,0,3,2:T(1,128)S(1)} %copy.83, s32[]{:T(128)S(6)} %copy.91, s32[]{:T(128)} %constant.119.clone.1..sunk, s32[]{:T(128)} %constant.119.clone.1..sunk, s32[]{:T(128)} %constant.119.clone.1..sunk) | dynamic-update-slice | bytes 786436 | tf_op jit(solution)/shard_map/while/body/jit(dynamic_update_index_in_dim)/dynamic_update_slice | solution.py:56
  64.7 2.2 %copy.73 = f32[24,8,2,512]{3,1,2,0:T(8,128)} copy(f32[24,8,2,512]{3,2,1,0:T(2,128)} %bitcast.129) | data formatting | bytes 1572864
  67.0 4.9 %select_reduce_fusion.2 = (bf16[64,4,48]{2,1,0:T(4,128)(2,1)S(1)}, bf16[64,4,48]{2,1,0:T(4,128)(2,1)S(1)}, bf16[64,4,48]{2,1,0:T(4,128)(2,1)S(1)}) fusion(bf16[64,16,4,48]{3,2,1,0:T(4,128)(2,1)S(1)} %copy-done.2, pred[16,4]{1,0:T(8,128)(4,1)S(1)} %iota_compare_fusion, bf16[64,16,4,48]{3,2,1,0:T(4,128)(2,1)} %reshape_reshape.26, ...), kind=kLoop, calls=%fused_computation.33 | loop fusion | flops 1142784 | bytes 1253440 | tf_op jit(solution)/shard_map/reduce_sum | solution.py:22
  72.2 14.0 %all_gather.6 = bf16[256,384]{1,0:T(8,128)(2,1)S(1)} all-gather(bf16[64,384]{1,0:T(8,128)(2,1)S(1)} %copy.58), channel_id=1, replica_groups=mesh['slides'=2,'seq'=4,'sub'=4] {'seq'}, dimensions={0}, use_global_device_ids=true | all-gather | bytes 245760 | tf_op jit(solution)/shard_map/all_gather | solution.py:118
  89.3 1.9 %broadcast_in_dim.318 = f32[1024,192]{1,0:T(8,128)} reshape(f32[64,16,4,48]{3,2,1,0:T(4,128)S(1)} %broadcast_in_dim.317) | data formatting | bytes 1572864 | tf_op jit(solution)/shard_map/jit(_where)/broadcast_in_dim | solution.py:32
  91.2 2.5 %copy.66 = f32[1024,192]{0,1:T(8,128)} copy(f32[1024,192]{1,0:T(8,128)} %broadcast_in_dim.318) | data formatting | bytes 1572864 | tf_op jit(solution)/shard_map/jit(_where)/broadcast_in_dim | solution.py:32
  97.9 13.9 %collective-permute-done.1 = bf16[512,384]{0,1:T(8,128)(2,1)S(1)} collective-permute-done((bf16[512,384]{0,1:T(8,128)(2,1)S(1)}, bf16[512,384]{0,1:T(8,128)(2,1)S(1)}, u32[]{:S(2)}, u32[]{:S(2)}) %collective-permute-start.1) | collective-permute-done | bytes 393248 | tf_op jit(solution)/shard_map/ppermute | solution.py:16
  113.7 1.7 %fusion.18 = f32[4,256]{1,0:T(4,128)} fusion(f32[4,256,1024]{2,1,0:T(8,128)S(1)} %get-tuple-element.185, f32[4,256]{1,0:T(4,128)S(1)} %get-tuple-element.184, pred[4,1024]{1,0:T(4,128)(4,1)S(1)} %add_compare_fusion), kind=kLoop, calls=%fused_computation.20 | loop fusion | flops 4193280 | bytes 4206592 | tf_op jit(solution)/shard_map/while/body/eval_jaxpr/reduce_sum | solution.py:50
  118.9 1.9 %broadcast_in_dim.313 = f32[1024,192]{1,0:T(8,128)} reshape(f32[256,4,4,48]{3,2,1,0:T(4,128)S(1)} %broadcast_in_dim.312) | data formatting | bytes 1572864 | tf_op jit(solution)/shard_map/jit(_where)/broadcast_in_dim | solution.py:32
  120.8 1.7 %copy.63 = f32[1024,192]{0,1:T(8,128)S(1)} copy(f32[1024,192]{1,0:T(8,128)} %broadcast_in_dim.313) | data formatting | bytes 1572864 | tf_op jit(solution)/shard_map/jit(_where)/broadcast_in_dim | solution.py:32
  122.5 1.7 %broadcast_in_dim.319 = f32[256,4,4]{1,0,2:T(8,128)} broadcast(f32[256,4]{0,1:T(4,128)} %bitcast.137), dimensions={0,2} | broadcast | bytes 20480 | tf_op jit(solution)/shard_map/jit(_where)/broadcast_in_dim | solution.py:31
  124.1 1.9 %broadcast_in_dim.320 = f32[1024,4]{0,1:T(4,128)} reshape(f32[256,4,4]{1,0,2:T(8,128)} %broadcast_in_dim.319) | data formatting | bytes 32768 | tf_op jit(solution)/shard_map/jit(_where)/broadcast_in_dim | solution.py:31
  127.0 1.9 %broadcast_in_dim.299 = f32[1024,4]{0,1:T(4,128)} reshape(f32[256,4,4]{1,0,2:T(8,128)} %broadcast_in_dim.298) | data formatting | bytes 32768 | tf_op jit(solution)/shard_map/jit(_where)/broadcast_in_dim | solution.py:30
  130.9 19.9 %all-gather.2.cloned.1.call-done = bf16[1024,768]{0,1:T(8,128)(2,1)} async-done(((bf16[1024,192]{0,1:T(8,128)(2,1)}), bf16[1024,768]{0,1:T(8,128)(2,1)}) %all-gather.2.cloned.1.call-update) | async-done | bytes 1572880 | tf_op jit(solution)/shard_map/all_gather | solution.py:144
  150.8 2.9 %fusion.23 = bf16[1024,192]{0,1:T(8,128)(2,1)} fusion(bf16[1024,768]{0,1:T(8,128)(2,1)} %all-gather.2.cloned.1.call-done, bf16[768,768]{1,0:T(8,128)(2,1)S(1)} %copy-done, s32[]{:T(128)S(6)} %select_n.145, pred[1024]{0:T(1024)(128)(4,1)S(1)} %get-tuple-element.278), kind=kOutput, calls=%fused_computation.25 | convolution fusion | flops 302383104 | bytes 2360324 | tf_op jit(solution)/shard_map/dot_general | solution.py:143
  (112 shorter events, 25.4 us)
Async XLA Ops:
  6.5 144.3 %copy-start = (bf16[768,768]{1,0:T(8,128)(2,1)S(1)}, bf16[768,768]{1,0:T(8,128)(2,1)}, u32[]{:S(2)}) copy-start(bf16[768,768]{1,0:T(8,128)(2,1)} %param.11) | copy-start | bytes 3538948
  6.5 144.3 %all-gather.2.cloned.1.call-start = ((), (), s32[]{:S(2)}) async-start(), calls=%async_computation | async-start | bytes 1966080 | tf_op jit(solution)/shard_map/all_gather | solution.py:144
  8.6 13.2 %copy-start.15 = (s32[4]{0:T(128)}, s32[4]{0:T(128)S(1)}, u32[]{:S(2)}) copy-start(s32[4]{0:T(128)S(1)} %get-tuple-element.180) | copy-start | bytes 52
  12.5 17.5 %copy-start.5 = (bf16[1024,192]{0,1:T(8,128)(2,1)S(1)}, bf16[1024,192]{0,1:T(8,128)(2,1)}, u32[]{:S(2)}) copy-start(bf16[1024,192]{0,1:T(8,128)(2,1)} %param.8) | copy-start | bytes 1179652
  12.5 3.1 %copy-start.17 = (pred[4,4]{1,0:T(4,128)(4,1)}, pred[4,4]{1,0:T(4,128)(4,1)S(1)}, u32[]{:S(2)}) copy-start(pred[4,4]{1,0:T(4,128)(4,1)S(1)} %iota_compare_fusion.1) | copy-start | bytes 52
  21.8 14.6 %copy-start.1 = (bf16[1024,192]{0,1:T(8,128)(2,1)S(1)}, bf16[1024,192]{0,1:T(8,128)(2,1)}, u32[]{:S(2)}) copy-start(bf16[1024,192]{0,1:T(8,128)(2,1)} %param.9) | copy-start | bytes 1179652
  21.8 13.8 %copy-start.18 = (pred[4,4]{1,0:T(4,128)(4,1)S(1)}, pred[4,4]{1,0:T(4,128)(4,1)}, u32[]{:S(2)}) copy-start(pred[4,4]{1,0:T(4,128)(4,1)} %copy-done.17) | copy-start | bytes 52
  27.0 66.9 %collective-permute-start = (bf16[256,384]{0,1:T(8,128)(2,1)}, bf16[256,384]{0,1:T(8,128)(2,1)}, u32[]{:S(2)}, u32[]{:S(2)}) collective-permute-start(bf16[256,384]{0,1:T(8,128)(2,1)} %pad_maximum_fusion.2), channel_id=1, source_target_pairs={{0,4},{4,0},{8,12},{12,8},{1,5},{5,1},{9,13},{13,9},{2,6},{6,2},{1... | collective-permute-start | bytes 589832 | tf_op jit(solution)/shard_map/ppermute | solution.py:16
  31.1 4.7 %copy-start.6 = (bf16[2,512,4,48]{1,0,3,2:T(2,128)(2,1)S(1)}, bf16[2,512,4,48]{1,0,3,2:T(2,128)(2,1)}, u32[]{:S(2)}) copy-start(bf16[2,512,4,48]{1,0,3,2:T(2,128)(2,1)} %reshape_reshape.21) | copy-start | bytes 1179652
  36.5 30.5 %copy-start.2 = (bf16[64,16,4,48]{3,2,1,0:T(4,128)(2,1)S(1)}, bf16[64,16,4,48]{3,2,1,0:T(4,128)(2,1)}, u32[]{:S(2)}) copy-start(bf16[64,16,4,48]{3,2,1,0:T(4,128)(2,1)} %reshape_reshape.25) | copy-start | bytes 1179652
  38.2 2.1 %copy-start.11 = (f32[2,512,4]{1,2,0:T(4,128)S(1)}, f32[2,512,4]{1,2,0:T(4,128)}, u32[]{:S(2)}) copy-start(f32[2,512,4]{1,2,0:T(4,128)} %get-tuple-element.254) | copy-start | bytes 49156 | tf_op jit(solution)/shard_map/while
  38.2 2.1 %copy-start.13 = (f32[2,512,4]{1,2,0:T(4,128)S(1)}, f32[2,512,4]{1,2,0:T(4,128)}, u32[]{:S(2)}) copy-start(f32[2,512,4]{1,2,0:T(4,128)} %get-tuple-element.255) | copy-start | bytes 49156 | tf_op jit(solution)/shard_map/while
  38.2 2.2 %copy-start.10 = (bf16[1024,4,48]{0,2,1:T(8,128)(2,1)S(1)}, bf16[1024,4,48]{0,2,1:T(8,128)(2,1)}, u32[]{:S(2)}) copy-start(bf16[1024,4,48]{0,2,1:T(8,128)(2,1)} %get-tuple-element.269) | copy-start | bytes 1179652 | tf_op jit(solution)/shard_map/while
  40.3 1.9 %copy-start.12 = (f32[2,512,4]{1,2,0:T(4,128)}, f32[2,512,4]{1,2,0:T(4,128)S(1)}, u32[]{:S(2)}) copy-start(f32[2,512,4]{1,2,0:T(4,128)S(1)} %get-tuple-element.264) | copy-start | bytes 49156 | tf_op jit(solution)/shard_map/while
  40.3 1.9 %copy-start.14 = (f32[2,512,4]{1,2,0:T(4,128)}, f32[2,512,4]{1,2,0:T(4,128)S(1)}, u32[]{:S(2)}) copy-start(f32[2,512,4]{1,2,0:T(4,128)S(1)} %get-tuple-element.265) | copy-start | bytes 49156 | tf_op jit(solution)/shard_map/while
  52.2 2.1 %copy-start.11 = (f32[2,512,4]{1,2,0:T(4,128)S(1)}, f32[2,512,4]{1,2,0:T(4,128)}, u32[]{:S(2)}) copy-start(f32[2,512,4]{1,2,0:T(4,128)} %get-tuple-element.254) | copy-start | bytes 49156 | tf_op jit(solution)/shard_map/while
  52.2 2.1 %copy-start.13 = (f32[2,512,4]{1,2,0:T(4,128)S(1)}, f32[2,512,4]{1,2,0:T(4,128)}, u32[]{:S(2)}) copy-start(f32[2,512,4]{1,2,0:T(4,128)} %get-tuple-element.255) | copy-start | bytes 49156 | tf_op jit(solution)/shard_map/while
  52.2 2.2 %copy-start.10 = (bf16[1024,4,48]{0,2,1:T(8,128)(2,1)S(1)}, bf16[1024,4,48]{0,2,1:T(8,128)(2,1)}, u32[]{:S(2)}) copy-start(bf16[1024,4,48]{0,2,1:T(8,128)(2,1)} %get-tuple-element.269) | copy-start | bytes 1179652 | tf_op jit(solution)/shard_map/while
  54.3 1.9 %copy-start.12 = (f32[2,512,4]{1,2,0:T(4,128)}, f32[2,512,4]{1,2,0:T(4,128)S(1)}, u32[]{:S(2)}) copy-start(f32[2,512,4]{1,2,0:T(4,128)S(1)} %get-tuple-element.264) | copy-start | bytes 49156 | tf_op jit(solution)/shard_map/while
  54.3 1.9 %copy-start.14 = (f32[2,512,4]{1,2,0:T(4,128)}, f32[2,512,4]{1,2,0:T(4,128)S(1)}, u32[]{:S(2)}) copy-start(f32[2,512,4]{1,2,0:T(4,128)S(1)} %get-tuple-element.265) | copy-start | bytes 49156 | tf_op jit(solution)/shard_map/while
  86.9 7.0 %copy-start.7 = (bf16[256,4,48]{0,2,1:T(8,128)(2,1)S(1)}, bf16[256,4,48]{0,2,1:T(8,128)(2,1)}, u32[]{:S(2)}) copy-start(bf16[256,4,48]{0,2,1:T(8,128)(2,1)} %copy.50) | copy-start | bytes 294916
  86.9 7.0 %copy-start.8 = (bf16[256,4,48]{0,2,1:T(8,128)(2,1)S(1)}, bf16[256,4,48]{0,2,1:T(8,128)(2,1)}, u32[]{:S(2)}) copy-start(bf16[256,4,48]{0,2,1:T(8,128)(2,1)} %copy.48) | copy-start | bytes 294916
  88.1 9.7 %copy-start.16 = (s32[4]{0:T(128)S(1)}, s32[4]{0:T(128)}, u32[]{:S(2)}) copy-start(s32[4]{0:T(128)} %copy-done.15) | copy-start | bytes 52
  91.2 21.7 %copy-start.9 = (bf16[256,4,48]{2,1,0:T(4,128)(2,1)S(1)}, bf16[256,4,48]{2,1,0:T(4,128)(2,1)}, u32[]{:S(2)}) copy-start(bf16[256,4,48]{2,1,0:T(4,128)(2,1)} %get-tuple-element.146) | copy-start | bytes 294916
  94.9 16.9 %collective-permute-start.1 = (bf16[512,384]{0,1:T(8,128)(2,1)S(1)}, bf16[512,384]{0,1:T(8,128)(2,1)S(1)}, u32[]{:S(2)}, u32[]{:S(2)}) collective-permute-start(bf16[512,384]{0,1:T(8,128)(2,1)S(1)} %pad_maximum_fusion.1), channel_id=1, source_target_pairs={{0,8},{4,12},{8,0},{12,4},{1,9},{5,13},{9,1},{13,5},{2,10},{6,14},... | collective-permute-start | bytes 1179656 | tf_op jit(solution)/shard_map/ppermute | solution.py:16
  120.8 9.0 %copy-start.3 = (f32[1024,192]{0,1:T(8,128)S(1)}, f32[1024,192]{0,1:T(8,128)}, u32[]{:S(2)}) copy-start(f32[1024,192]{0,1:T(8,128)} %copy.66) | copy-start | bytes 2359300
  120.8 9.0 %copy-start.4 = (f32[24,8,2,512]{3,1,2,0:T(8,128)S(1)}, f32[24,8,2,512]{3,1,2,0:T(8,128)}, u32[]{:S(2)}) copy-start(f32[24,8,2,512]{3,1,2,0:T(8,128)} %copy.73) | copy-start | bytes 2359300
Sparse Core Ops, SparseCore 0:
  131.0 19.7 all-gather.1
where the time goes:
time: 162 us; the launch traced here: 161 us
  local copies, waits for them, and re-layouts  59.1 us (36%)
  waiting for transfers between devices  33.8 us (21%)
  other arithmetic  23.1 us (14%)
  between operations  14.3 us (9%)
  blocking collectives  14 us (9%)
  matrix products  12 us (7%)
  starting transfers between devices  3.75 us (2%)
    all_gather x1, waiting for transfers between devices, local(): lax.all_gather(attn, 'sub', axis=1, tiled=True)  19.9 us
    dynamic_update_slice x6, local copies, waits for them, and re-layouts, block_stats(): lax.map(attend, q_sel.reshape(n_query // width, width, q_sel.shape[1], q_...  17 us
    all_gather x1, blocking collectives, local(): piece = lax.all_gather(kv_wide, 'seq', axis=0, tiled=True)  14 us
    ppermute x2, waiting for transfers between devices, swapped(): return lax.ppermute(value, axis, pairs)  13.9 us
    reduce_sum x2, other arithmetic, pick_rows(): jnp.sum(jnp.where(onehot[None, :, :, None], grouped, jnp.zeros((), source...  11.1 us
    broadcast_in_dim x6, local copies, waits for them, and re-layouts, spread_back(): jnp.where(onehot[..., None], numer[:, None, :, :], 0.0)  10.4 us
    another operation x6, local copies, waits for them, and re-layouts, pick_rows(): source.reshape(source.shape[0] // stride, stride, source.shape[1], source...  9.14 us
    reduce_sum x4, other arithmetic, attend(): mass = jnp.sum(probs, axis=2)  6.02 us
  transfers between devices with their start and end apart: 3, of which 2 were waited for; matrix products, arithmetic and copies ran while one was open for 32% of the time, Pallas kernels for 0%

commit v1 on v0

--- a/solution.py
+++ b/solution.py
@@ -115,7 +115,13 @@
         ],
         axis=1,
     )
-    piece = lax.all_gather(kv_wide, "seq", axis=0, tiled=True)
+    count_2 = lax.axis_size("seq")
+    held, parts = (kv_wide, [kv_wide])
+    for _ in range(count_2 - 1):
+        held = lax.ppermute(held, "seq", [(i, (i + 1) % count_2) for i in range(count_2)])
+        parts.insert(0, held)
+    line = jnp.concatenate(parts, axis=0)
+    piece = jnp.roll(line, (lax.axis_index("seq") + 1) * kv_wide.shape[0], axis=0)
     run_peak = jnp.full((wide_rows, local_heads), NEG_FILL, jnp.float32)
     piece_len = piece.shape[0]
     global_row = jnp.arange(piece_len, dtype=jnp.int32)

time: 162 us -> 142 us (0.88)
  blocking collectives: 14 us -> 0 us
  local copies, waits for them, and re-layouts: 59.1 us -> 50.2 us
  waiting for transfers between devices: 33.8 us -> 36.5 us
  starting transfers between devices: 3.75 us -> 5.37 us
    all_gather x1 -> x0, blocking collectives: 14 us -> none  [local(): piece = lax.all_gather(kv_wide, 'seq', axis=0, tiled=True)]
    ppermute x0 -> x3, waiting for transfers between devices: none -> 8.42 us  [local(): lax.ppermute(held, 'seq', [(i, (i + 1) % count_2) for i in range(count_2)])]
    dynamic_update_slice x6, local copies, waits for them, and re-layouts: 17 us -> 9.32 us  [block_stats(): lax.map(attend, q_sel.reshape(n_query // width, width, q_sel.shape[1], q_...]
    ppermute x2, waiting for transfers between devices: 13.9 us -> 9.21 us  [swapped(): return lax.ppermute(value, axis, pairs)]
    ppermute x0 -> x3, starting transfers between devices: none -> 3.79 us  [local(): lax.ppermute(held, 'seq', [(i, (i + 1) % count_2) for i in range(count_2)])]
    reduce_sum x4, local copies, waits for them, and re-layouts: 3.72 us -> 0.51 us  [pick_rows(): jnp.sum(jnp.where(onehot[None, :, :, None], grouped, jnp.zeros((), source...]
    ppermute x2, starting transfers between devices: 3.75 us -> 1.58 us  [swapped(): return lax.ppermute(value, axis, pairs)]
    while x20 -> x12, local copies, waits for them, and re-layouts: 0.05 us -> 1.78 us
  transfers between devices with their start and end apart: 3 -> 6, of which waited for: 2 -> 4; matrix products, arithmetic and copies ran while one was open for 32% -> 33% of each run, Pallas kernels for 0% -> 0%
where the time goes in v1:
time: 142 us
  local copies, waits for them, and re-layouts  50.2 us (35%)
  waiting for transfers between devices  36.5 us (26%)
  other arithmetic  23.1 us (16%)
  between operations  14.3 us (10%)
  matrix products  12 us (8%)
  starting transfers between devices  5.37 us (4%)
    all_gather x1, waiting for transfers between devices, local(): lax.all_gather(attn, 'sub', axis=1, tiled=True)  18.8 us
    reduce_sum x2, other arithmetic, pick_rows(): jnp.sum(jnp.where(onehot[None, :, :, None], grouped, jnp.zeros((), source...  11.2 us
    broadcast_in_dim x6, local copies, waits for them, and re-layouts, spread_back(): jnp.where(onehot[..., None], numer[:, None, :, :], 0.0)  10.4 us
    dynamic_update_slice x6, local copies, waits for them, and re-layouts, block_stats(): lax.map(attend, q_sel.reshape(n_query // width, width, q_sel.shape[1], q_...  9.32 us
    ppermute x2, waiting for transfers between devices, swapped(): return lax.ppermute(value, axis, pairs)  9.21 us
    another operation x6, local copies, waits for them, and re-layouts, pick_rows(): source.reshape(source.shape[0] // stride, stride, source.shape[1], source...  8.97 us
    ppermute x3, waiting for transfers between devices, local(): lax.ppermute(held, 'seq', [(i, (i + 1) % count_2) for i in range(count_2)])  8.42 us
    reduce_sum x4, other arithmetic, attend(): mass = jnp.sum(probs, axis=2)  6.04 us
  transfers between devices with their start and end apart: 6, of which 4 were waited for; matrix products, arithmetic and copies ran while one was open for 33% of the time, Pallas kernels for 0%

profile of v1, /device:TPU:0, one launch (start us, length us, event | category | flops | bytes accessed | tf_op | source)
XLA Modules:
  0.0 141.7 jit_solution(106446940967610746)
XLA Ops:
  7.9 1.5 %reshape_reshape.25 = bf16[64,16,4,48]{3,2,1,0:T(4,128)(2,1)} reshape(bf16[1024,192]{1,0:T(8,128)(2,1)S(1)} %copy.46) | data formatting | bytes 786432 | tf_op jit(solution)/shard_map/reshape;reshape | solution.py:20
  11.3 1.5 %reshape_reshape.26 = bf16[64,16,4,48]{3,2,1,0:T(4,128)(2,1)} reshape(bf16[1024,192]{1,0:T(8,128)(2,1)S(1)} %copy.47) | data formatting | bytes 786432 | tf_op jit(solution)/shard_map/reshape;reshape | solution.py:20
  13.0 1.5 %reshape_reshape.27 = bf16[64,16,4,48]{3,2,1,0:T(4,128)(2,1)} reshape(bf16[1024,192]{1,0:T(8,128)(2,1)S(1)} %copy.49) | data formatting | bytes 786432 | tf_op jit(solution)/shard_map/reshape;reshape | solution.py:20
  14.5 5.2 %select_reduce_fusion.2 = (bf16[64,4,48]{2,1,0:T(4,128)(2,1)S(1)}, bf16[64,4,48]{2,1,0:T(4,128)(2,1)S(1)}, bf16[64,4,48]{2,1,0:T(4,128)(2,1)S(1)}) fusion(bf16[64,16,4,48]{3,2,1,0:T(4,128)(2,1)} %reshape_reshape.25, pred[16,4]{1,0:T(8,128)(4,1)S(1)} %iota_compare_fusion, bf16[64,16,4,48]{3,2,1,0:T(4,128)(2,1)} %reshape_reshape.26, ...), kind=kLoop, calls=%fused_computation.33 | loop fusion | flops 1142784 | bytes 1253440 | tf_op jit(solution)/shard_map/reduce_sum | solution.py:22
  20.0 3.3 %collective-permute-start.2 = (bf16[64,384]{0,1:T(8,128)(2,1)S(1)}, bf16[64,384]{0,1:T(8,128)(2,1)}, u32[]{:S(2)}, u32[]{:S(2)}) collective-permute-start(bf16[64,384]{0,1:T(8,128)(2,1)S(1)} %pad_maximum_fusion.3), channel_id=1, source_target_pairs={{0,4},{4,8},{8,12},{12,0},{1,5},{5,9},{9,13},{13,1},{2,6},{6,10},{... | collective-permute-start | bytes 147464 | tf_op jit(solution)/shard_map/ppermute | solution.py:121
  23.3 1.5 %reshape_reshape.22 = bf16[256,4,4,48]{3,2,1,0:T(4,128)(2,1)} reshape(bf16[1024,192]{1,0:T(8,128)(2,1)S(1)} %copy.46) | data formatting | bytes 786432 | tf_op jit(solution)/shard_map/reshape;reshape | solution.py:20
  26.3 1.5 %reshape_reshape.24 = bf16[256,4,4,48]{3,2,1,0:T(4,128)(2,1)} reshape(bf16[1024,192]{1,0:T(8,128)(2,1)S(1)} %copy.49) | data formatting | bytes 786432 | tf_op jit(solution)/shard_map/reshape;reshape | solution.py:20
  27.8 6.0 %select_reduce_fusion.5 = (bf16[256,4,48]{2,1,0:T(4,128)(2,1)}, bf16[256,4,48]{2,1,0:T(4,128)(2,1)S(1)}, bf16[256,4,48]{2,1,0:T(4,128)(2,1)S(1)}) fusion(bf16[256,4,4,48]{3,2,1,0:T(4,128)(2,1)} %reshape_reshape.22, pred[4,4]{1,0:T(4,128)(4,1)S(1)} %iota_compare_fusion.1, bf16[256,4,4,48]{3,2,1,0:T(4,128)(2,1)} %reshape_reshape.23, ...), kind=kLoop, calls=%fused_computation.36 | loop fusion | flops 1032192 | bytes 1474576 | tf_op jit(solution)/shard_map/reduce_sum | solution.py:22
  34.8 1.6 %collective-permute-start = (bf16[256,384]{0,1:T(8,128)(2,1)}, bf16[256,384]{0,1:T(8,128)(2,1)}, u32[]{:S(2)}, u32[]{:S(2)}) collective-permute-start(bf16[256,384]{0,1:T(8,128)(2,1)} %pad_maximum_fusion.2), channel_id=1, source_target_pairs={{0,4},{4,0},{8,12},{12,8},{1,5},{5,1},{9,13},{13,9},{2,6},{6,2},{1... | collective-permute-start | bytes 589832 | tf_op jit(solution)/shard_map/ppermute | solution.py:16
  37.4 22.0 %while.3 = (s32[]{:T(128)}, f32[2,512,4]{1,2,0:T(4,128)S(1)}, f32[2,512,4]{1,2,0:T(4,128)}, f32[2,512,4,48]{1,0,3,2:T(2,128)}, bf16[2,512,4,48]{1,3,2,0:T(8,128)...) while((s32[]{:T(128)}, f32[2,512,4]{1,2,0:T(4,128)S(1)}, ...), condition=%wide.region_3.4_spmd.clone, body=%wide.region_0.3_spmd.clone.sunk | while | flops 425717760 | bytes 36048076 | solution.py:56
  37.5 1.5 %fusion.67 = (f32[4,512]{1,0:T(4,128)S(1)}, f32[4,512,1024]{2,1,0:T(8,128)S(1)}) fusion(pred[1024]{0:T(1024)(128)(4,1)S(1)} %get-tuple-element.270, bf16[1024,4,48]{0,2,1:T(8,128)(2,1)S(1)} %get-tuple-element.268, bf16[2,512,4,48]{1,3,2,0:T(8,128)(2,1)S(1)} %get-tuple-element.267, s32[]{:T(128)S(6)} %copy.88), kind=kOutput, calls=%fused_computation.3.clone.1 | convolution fusion | flops 207616000 | bytes 8987652 | tf_op jit(solution)/shard_map/while/body/eval_jaxpr/qhd,khd->hqk/dot_general | solution.py:44
  38.9 2.1 %fusion.68 = f32[4,512]{1,0:T(4,128)S(1)} fusion(f32[4,512,1024]{2,1,0:T(8,128)S(1)} %get-tuple-element.239, f32[4,512]{1,0:T(4,128)S(1)} %get-tuple-element.240, pred[1024]{0:T(1024)(128)(4,1)S(1)} %get-tuple-element.270), kind=kLoop, calls=%fused_computation.5.clone.1 | loop fusion | flops 8386560 | bytes 8406016 | tf_op jit(solution)/shard_map/while/body/eval_jaxpr/reduce_sum | solution.py:50
  41.6 1.8 %fusion.69 = f32[1,512,4,48]{1,3,2,0:T(8,128)S(1)} fusion(bf16[1024,4,48]{0,2,1:T(8,128)(2,1)S(1)} %copy-done.9, f32[4,512,1024]{2,1,0:T(8,128)S(1)} %get-tuple-element.239, f32[4,512]{1,0:T(4,128)S(1)} %get-tuple-element.240, pred[1024]{0:T(1024)(128)(4,1)S(1)} %get-tuple-element.270), kind=kOutput, calls=%fused_computation.8.clone.1 | convolution fusion | flops 209715200 | bytes 9184256 | tf_op jit(solution)/shard_map/while/body/eval_jaxpr/hqk,khd->qhd/dot_general | solution.py:51
  43.9 3.6 %dynamic_update_slice.35 = f32[2,512,4,48]{1,0,3,2:T(2,128)S(1)} dynamic-update-slice(f32[2,512,4,48]{1,0,3,2:T(2,128)S(1)} %copy-done.6, f32[1,512,4,48]{1,0,3,2:T(1,128)S(1)} %copy.80, s32[]{:T(128)S(6)} %copy.88, s32[]{:T(128)} %constant.138.clone.1..sunk, s32[]{:T(128)} %constant.138.clone.1..sunk, s32[]{:T(128)} %constant.138.clone.1..sunk) | dynamic-update-slice | bytes 786436 | tf_op jit(solution)/shard_map/while/body/jit(dynamic_update_index_in_dim)/dynamic_update_slice | solution.py:56
  50.0 2.1 %fusion.68 = f32[4,512]{1,0:T(4,128)S(1)} fusion(f32[4,512,1024]{2,1,0:T(8,128)S(1)} %get-tuple-element.239, f32[4,512]{1,0:T(4,128)S(1)} %get-tuple-element.240, pred[1024]{0:T(1024)(128)(4,1)S(1)} %get-tuple-element.270), kind=kLoop, calls=%fused_computation.5.clone.1 | loop fusion | flops 8386560 | bytes 8406016 | tf_op jit(solution)/shard_map/while/body/eval_jaxpr/reduce_sum | solution.py:50
  52.6 1.8 %fusion.69 = f32[1,512,4,48]{1,3,2,0:T(8,128)S(1)} fusion(bf16[1024,4,48]{0,2,1:T(8,128)(2,1)S(1)} %copy-done.9, f32[4,512,1024]{2,1,0:T(8,128)S(1)} %get-tuple-element.239, f32[4,512]{1,0:T(4,128)S(1)} %get-tuple-element.240, pred[1024]{0:T(1024)(128)(4,1)S(1)} %get-tuple-element.270), kind=kOutput, calls=%fused_computation.8.clone.1 | convolution fusion | flops 209715200 | bytes 9184256 | tf_op jit(solution)/shard_map/while/body/eval_jaxpr/hqk,khd->qhd/dot_general | solution.py:51
  54.9 3.6 %dynamic_update_slice.35 = f32[2,512,4,48]{1,0,3,2:T(2,128)S(1)} dynamic-update-slice(f32[2,512,4,48]{1,0,3,2:T(2,128)S(1)} %copy-done.6, f32[1,512,4,48]{1,0,3,2:T(1,128)S(1)} %copy.80, s32[]{:T(128)S(6)} %copy.88, s32[]{:T(128)} %constant.138.clone.1..sunk, s32[]{:T(128)} %constant.138.clone.1..sunk, s32[]{:T(128)} %constant.138.clone.1..sunk) | dynamic-update-slice | bytes 786436 | tf_op jit(solution)/shard_map/while/body/jit(dynamic_update_index_in_dim)/dynamic_update_slice | solution.py:56
  60.3 6.2 %collective-permute-done.3 = bf16[64,384]{0,1:T(8,128)(2,1)S(1)} collective-permute-done((bf16[64,384]{0,1:T(8,128)(2,1)}, bf16[64,384]{0,1:T(8,128)(2,1)S(1)}, u32[]{:S(2)}, u32[]{:S(2)}) %collective-permute-start.3) | collective-permute-done | bytes 49184 | tf_op jit(solution)/shard_map/ppermute | solution.py:121
  67.3 2.2 %copy.70 = f32[24,8,2,512]{3,1,2,0:T(8,128)} copy(f32[24,8,2,512]{3,2,1,0:T(2,128)} %bitcast.129) | data formatting | bytes 1572864
  70.6 2.2 %collective-permute-done.4 = bf16[64,384]{0,1:T(8,128)(2,1)S(1)} collective-permute-done((bf16[64,384]{0,1:T(8,128)(2,1)S(1)}, bf16[64,384]{0,1:T(8,128)(2,1)S(1)}, u32[]{:S(2)}, u32[]{:S(2)}) %collective-permute-start.4) | collective-permute-done | bytes 49184 | tf_op jit(solution)/shard_map/ppermute | solution.py:121
  74.7 1.7 %pad_maximum_fusion.1 = bf16[512,384]{0,1:T(8,128)(2,1)} fusion(bf16[256,384]{0,1:T(8,128)(2,1)} %collective-permute-done, bf16[256,192]{0,1:T(8,128)(2,1)S(1)} %bitcast.124, bf16[256,192]{0,1:T(8,128)(2,1)S(1)} %bitcast.127), kind=kLoop, calls=%fused_computation.45 | loop fusion | flops 1179648 | bytes 786432 | tf_op jit(solution)/shard_map/concatenate | solution.py:94
  78.6 1.9 %broadcast_in_dim.318 = f32[1024,192]{1,0:T(8,128)} reshape(f32[64,16,4,48]{3,2,1,0:T(4,128)S(1)} %broadcast_in_dim.317) | data formatting | bytes 1572864 | tf_op jit(solution)/shard_map/jit(_where)/broadcast_in_dim | solution.py:32
  80.5 2.5 %copy.63 = f32[1024,192]{0,1:T(8,128)} copy(f32[1024,192]{1,0:T(8,128)} %broadcast_in_dim.318) | data formatting | bytes 1572864 | tf_op jit(solution)/shard_map/jit(_where)/broadcast_in_dim | solution.py:32
  84.6 9.2 %collective-permute-done.1 = bf16[512,384]{0,1:T(8,128)(2,1)} collective-permute-done((bf16[512,384]{0,1:T(8,128)(2,1)}, bf16[512,384]{0,1:T(8,128)(2,1)}, u32[]{:S(2)}, u32[]{:S(2)}) %collective-permute-start.1) | collective-permute-done | bytes 393248 | tf_op jit(solution)/shard_map/ppermute | solution.py:16
  95.9 1.7 %fusion.18 = f32[4,256]{1,0:T(4,128)} fusion(f32[4,256,1024]{2,1,0:T(8,128)S(1)} %get-tuple-element.185, f32[4,256]{1,0:T(4,128)S(1)} %get-tuple-element.184, pred[4,1024]{1,0:T(4,128)(4,1)S(1)} %add_compare_fusion), kind=kLoop, calls=%fused_computation.20 | loop fusion | flops 4193280 | bytes 4206592 | tf_op jit(solution)/shard_map/while/body/eval_jaxpr/reduce_sum | solution.py:50
  101.1 1.9 %broadcast_in_dim.313 = f32[1024,192]{1,0:T(8,128)} reshape(f32[256,4,4,48]{3,2,1,0:T(4,128)S(1)} %broadcast_in_dim.312) | data formatting | bytes 1572864 | tf_op jit(solution)/shard_map/jit(_where)/broadcast_in_dim | solution.py:32
  103.0 1.7 %copy.61 = f32[1024,192]{0,1:T(8,128)S(1)} copy(f32[1024,192]{1,0:T(8,128)} %broadcast_in_dim.313) | data formatting | bytes 1572864 | tf_op jit(solution)/shard_map/jit(_where)/broadcast_in_dim | solution.py:32
  104.7 1.7 %broadcast_in_dim.319 = f32[256,4,4]{1,0,2:T(8,128)} broadcast(f32[256,4]{0,1:T(4,128)} %bitcast.137), dimensions={0,2} | broadcast | bytes 20480 | tf_op jit(solution)/shard_map/jit(_where)/broadcast_in_dim | solution.py:31
  106.3 1.9 %broadcast_in_dim.320 = f32[1024,4]{0,1:T(4,128)} reshape(f32[256,4,4]{1,0,2:T(8,128)} %broadcast_in_dim.319) | data formatting | bytes 32768 | tf_op jit(solution)/shard_map/jit(_where)/broadcast_in_dim | solution.py:31
  109.3 1.9 %broadcast_in_dim.299 = f32[1024,4]{0,1:T(4,128)} reshape(f32[256,4,4]{1,0,2:T(8,128)} %broadcast_in_dim.298) | data formatting | bytes 32768 | tf_op jit(solution)/shard_map/jit(_where)/broadcast_in_dim | solution.py:30
  113.2 18.8 %all-gather.2.cloned.1.call-done = bf16[1024,768]{0,1:T(8,128)(2,1)} async-done(((bf16[1024,192]{0,1:T(8,128)(2,1)}), bf16[1024,768]{0,1:T(8,128)(2,1)}) %all-gather.2.cloned.1.call-update) | async-done | bytes 1572880 | tf_op jit(solution)/shard_map/all_gather | solution.py:150
  132.0 2.9 %fusion.23 = bf16[1024,192]{0,1:T(8,128)(2,1)} fusion(bf16[1024,768]{0,1:T(8,128)(2,1)} %all-gather.2.cloned.1.call-done, bf16[768,768]{1,0:T(8,128)(2,1)S(1)} %copy-done, s32[]{:T(128)S(6)} %select_n.159, pred[1024]{0:T(1024)(128)(4,1)S(1)} %get-tuple-element.280), kind=kOutput, calls=%fused_computation.25 | convolution fusion | flops 302383104 | bytes 2360324 | tf_op jit(solution)/shard_map/dot_general | solution.py:149
  (103 shorter events, 28.7 us)
Async XLA Ops:
  6.5 125.4 %copy-start = (bf16[768,768]{1,0:T(8,128)(2,1)S(1)}, bf16[768,768]{1,0:T(8,128)(2,1)}, u32[]{:S(2)}) copy-start(bf16[768,768]{1,0:T(8,128)(2,1)} %param.11) | copy-start | bytes 3538948
  6.5 6.3 %copy-start.8 = (bf16[1024,192]{0,1:T(8,128)(2,1)S(1)}, bf16[1024,192]{0,1:T(8,128)(2,1)}, u32[]{:S(2)}) copy-start(bf16[1024,192]{0,1:T(8,128)(2,1)} %param.10) | copy-start | bytes 1179652
  6.5 125.4 %all-gather.2.cloned.1.call-start = ((), (), s32[]{:S(2)}) async-start(), calls=%async_computation | async-start | bytes 1966080 | tf_op jit(solution)/shard_map/all_gather | solution.py:150
  10.1 17.6 %copy-start.12 = (s32[4]{0:T(128)}, s32[4]{0:T(128)S(1)}, u32[]{:S(2)}) copy-start(s32[4]{0:T(128)S(1)} %get-tuple-element.180) | copy-start | bytes 52
  20.0 39.8 %collective-permute-start.2 = (bf16[64,384]{0,1:T(8,128)(2,1)S(1)}, bf16[64,384]{0,1:T(8,128)(2,1)}, u32[]{:S(2)}, u32[]{:S(2)}) collective-permute-start(bf16[64,384]{0,1:T(8,128)(2,1)S(1)} %pad_maximum_fusion.3), channel_id=1, source_target_pairs={{0,4},{4,8},{8,12},{12,0},{1,5},{5,9},{9,13},{13,1},{2,6},{6,10},{... | collective-permute-start | bytes 147464 | tf_op jit(solution)/shard_map/ppermute | solution.py:121
  24.8 11.6 %copy-start.4 = (bf16[1024,192]{0,1:T(8,128)(2,1)S(1)}, bf16[1024,192]{0,1:T(8,128)(2,1)}, u32[]{:S(2)}) copy-start(bf16[1024,192]{0,1:T(8,128)(2,1)} %param.8) | copy-start | bytes 1179652
  26.3 11.2 %copy-start.1 = (bf16[1024,192]{0,1:T(8,128)(2,1)S(1)}, bf16[1024,192]{0,1:T(8,128)(2,1)}, u32[]{:S(2)}) copy-start(bf16[1024,192]{0,1:T(8,128)(2,1)} %param.9) | copy-start | bytes 1179652
  27.8 9.7 %copy-start.14 = (pred[4,4]{1,0:T(4,128)(4,1)}, pred[4,4]{1,0:T(4,128)(4,1)S(1)}, u32[]{:S(2)}) copy-start(pred[4,4]{1,0:T(4,128)(4,1)S(1)} %iota_compare_fusion.1) | copy-start | bytes 52
  34.8 39.9 %collective-permute-start = (bf16[256,384]{0,1:T(8,128)(2,1)}, bf16[256,384]{0,1:T(8,128)(2,1)}, u32[]{:S(2)}, u32[]{:S(2)}) collective-permute-start(bf16[256,384]{0,1:T(8,128)(2,1)} %pad_maximum_fusion.2), channel_id=1, source_target_pairs={{0,4},{4,0},{8,12},{12,8},{1,5},{5,1},{9,13},{13,9},{2,6},{6,2},{1... | collective-permute-start | bytes 589832 | tf_op jit(solution)/shard_map/ppermute | solution.py:16
  37.4 22.3 %copy-start.13 = (s32[4]{0:T(128)S(1)}, s32[4]{0:T(128)}, u32[]{:S(2)}) copy-start(s32[4]{0:T(128)} %copy-done.12) | copy-start | bytes 52
  38.9 2.7 %copy-start.9 = (bf16[1024,4,48]{0,2,1:T(8,128)(2,1)S(1)}, bf16[1024,4,48]{0,2,1:T(8,128)(2,1)}, u32[]{:S(2)}) copy-start(bf16[1024,4,48]{0,2,1:T(8,128)(2,1)} %get-tuple-element.269) | copy-start | bytes 1179652 | tf_op jit(solution)/shard_map/while
  41.6 2.3 %copy-start.6 = (f32[2,512,4,48]{1,0,3,2:T(2,128)S(1)}, f32[2,512,4,48]{1,0,3,2:T(2,128)}, u32[]{:S(2)}) copy-start(f32[2,512,4,48]{1,0,3,2:T(2,128)} %get-tuple-element.256) | copy-start | bytes 2359300 | tf_op jit(solution)/shard_map/while
  47.6 0.9 copy-start.7
  49.9 2.7 %copy-start.9 = (bf16[1024,4,48]{0,2,1:T(8,128)(2,1)S(1)}, bf16[1024,4,48]{0,2,1:T(8,128)(2,1)}, u32[]{:S(2)}) copy-start(bf16[1024,4,48]{0,2,1:T(8,128)(2,1)} %get-tuple-element.269) | copy-start | bytes 1179652 | tf_op jit(solution)/shard_map/while
  52.6 2.3 %copy-start.6 = (f32[2,512,4,48]{1,0,3,2:T(2,128)S(1)}, f32[2,512,4,48]{1,0,3,2:T(2,128)}, u32[]{:S(2)}) copy-start(f32[2,512,4,48]{1,0,3,2:T(2,128)} %get-tuple-element.256) | copy-start | bytes 2359300 | tf_op jit(solution)/shard_map/while
  58.6 0.9 copy-start.7
  59.5 10.0 %copy-start.11 = (f32[2,512,4]{1,2,0:T(4,128)}, f32[2,512,4]{1,2,0:T(4,128)S(1)}, u32[]{:S(2)}) copy-start(f32[2,512,4]{1,2,0:T(4,128)S(1)} %get-tuple-element.87) | copy-start | bytes 49156
  59.8 6.7 %collective-permute-start.3 = (bf16[64,384]{0,1:T(8,128)(2,1)}, bf16[64,384]{0,1:T(8,128)(2,1)S(1)}, u32[]{:S(2)}, u32[]{:S(2)}) collective-permute-start(bf16[64,384]{0,1:T(8,128)(2,1)} %collective-permute-done.2), channel_id=1, source_target_pairs={{0,4},{4,8},{8,12},{12,0},{1,5},{5,9},{9,13},{13,1},{2,6},{6,10},{... | collective-permute-start | bytes 147464 | tf_op jit(solution)/shard_map/ppermute | solution.py:121
  66.5 6.4 %collective-permute-start.4 = (bf16[64,384]{0,1:T(8,128)(2,1)S(1)}, bf16[64,384]{0,1:T(8,128)(2,1)S(1)}, u32[]{:S(2)}, u32[]{:S(2)}) collective-permute-start(bf16[64,384]{0,1:T(8,128)(2,1)S(1)} %collective-permute-done.3), channel_id=1, source_target_pairs={{0,4},{4,8},{8,12},{12,0},{1,5},{5,9},{9,13},{13,1},{2,6},{6,10},{... | collective-permute-start | bytes 147464 | tf_op jit(solution)/shard_map/ppermute | solution.py:121
  76.4 17.4 %collective-permute-start.1 = (bf16[512,384]{0,1:T(8,128)(2,1)}, bf16[512,384]{0,1:T(8,128)(2,1)}, u32[]{:S(2)}, u32[]{:S(2)}) collective-permute-start(bf16[512,384]{0,1:T(8,128)(2,1)} %pad_maximum_fusion.1), channel_id=1, source_target_pairs={{0,8},{4,12},{8,0},{12,4},{1,9},{5,13},{9,1},{13,5},{2,10},{6,14},... | collective-permute-start | bytes 1179656 | tf_op jit(solution)/shard_map/ppermute | solution.py:16
  80.5 14.5 %copy-start.5 = (bf16[256,4,48]{2,1,0:T(4,128)(2,1)S(1)}, bf16[256,4,48]{2,1,0:T(4,128)(2,1)}, u32[]{:S(2)}) copy-start(bf16[256,4,48]{2,1,0:T(4,128)(2,1)} %get-tuple-element.146) | copy-start | bytes 294916
  101.1 10.1 %copy-start.10 = (pred[1024,4]{0,1:T(4,128)(4,1)S(1)}, pred[1024,4]{0,1:T(4,128)(4,1)}, u32[]{:S(2)}) copy-start(pred[1024,4]{0,1:T(4,128)(4,1)} %broadcast_in_dim.293) | copy-start | bytes 12292
  103.0 9.1 %copy-start.2 = (f32[1024,192]{0,1:T(8,128)S(1)}, f32[1024,192]{0,1:T(8,128)}, u32[]{:S(2)}) copy-start(f32[1024,192]{0,1:T(8,128)} %copy.63) | copy-start | bytes 2359300
  103.0 9.1 %copy-start.3 = (f32[24,8,2,512]{3,1,2,0:T(8,128)S(1)}, f32[24,8,2,512]{3,1,2,0:T(8,128)}, u32[]{:S(2)}) copy-start(f32[24,8,2,512]{3,1,2,0:T(8,128)} %copy.70) | copy-start | bytes 2359300
Sparse Core Ops, SparseCore 0:
  113.3 18.6 all-gather.1
